TPU v7x, 32 devices: a whole 2x2x4 slice. The times are simulated.
32 devices in a mesh: row: 8 (over z, y), col: 4 (over x, core).
Axes of the slice: x: 2, y: 2, z: 4, core: 2. Of those that a mesh axis runs over, the one named last changes fastest.
Arguments:
- eigvec: float32 [32, 8, 128, 1024], P(None, 'row', None, 'col'), may hold values from -6 to 6
- reflectors: float32 [2, 32, 8, 256, 128], P(None, None, 'row', 'col'), may hold values from -6 to 6
- sweep_group: int32 [2, 32, 8], P(None, None, 'row'), may hold values from -1 to 254, as said below
Outputs:
- transformed: float32 [32, 8, 128, 1024], P(None, 'row', None, 'col')
Inputs may be any that keep to these rules, and one draw needn't show every extreme that they name: `sweep_group`: -1 where no diamond sits at that diagonal and tile position (tile position l * R + r for entry [d, l, r]); otherwise the diamond's sweep group, at most its tile position. Within one diagonal no two diamonds sit at adjacent tile positions, and none sits at the last tile position 255.
All inputs are finite; a program needn't handle non-finite values.
Results may differ from a plain program's by a relative error of at most 0.0003.
Values sent between devices are 32-bit elements.
A program may use at most 128 MiB of HBM per device.

v0:
```python
import functools

import jax
import jax.numpy as jnp
from jax import lax
from jax.experimental import pallas as pl
from jax.experimental.pallas import tpu as pltpu
from jax.sharding import PartitionSpec as P


SLOT_SIZES = (10, 12, 14, 16)
GROUP = 2
CHUNKS = 2


def split(x):
    high = x.astype(jnp.bfloat16)
    return high, (x - high.astype(jnp.float32)).astype(jnp.bfloat16)


def dot(a, b):
    return jnp.dot(a, b, preferred_element_type=jnp.float32)


def dot3(a, b):
    return dot(a[1], b[0]) + dot(a[0], b[1]) + dot(a[0], b[0])


def bounds(slots):
    return [slots * i // CHUNKS for i in range(CHUNKS + 1)]


def chunk_shapes(slots, tiles):
    edges = bounds(slots)
    return [
        jax.ShapeDtypeStruct((high - low,) + tiles.shape[1:], tiles.dtype)
        for low, high in zip(edges[:-1], edges[1:])
    ]


def slot_of(chunks, k):
    for chunk in chunks:
        if k < chunk.shape[0]:
            return chunk.at[k]
        k -= chunk.shape[0]


def gather_kernel(slots, own, behind, panels, tiles, picked, *rest):
    diagonals = panels.shape[0]
    sent, sems = rest[:-1], rest[-1]

    def panel_copy(d, k):
        return pltpu.make_async_copy(
            panels.at[d, own[d, k]], picked.at[d, k], sems.at[d * slots + k]
        )

    def tile_copy(k):
        return pltpu.make_async_copy(
            tiles.at[behind[0, k]], slot_of(sent, k), sems.at[diagonals * slots + k]
        )

    for k in range(slots):
        tile_copy(k).start()
    for d in range(diagonals):
        for k in range(slots):
            panel_copy(d, k).start()
    for k in range(slots):
        tile_copy(k).wait()
    for d in range(diagonals):
        for k in range(slots):
            panel_copy(d, k).wait()


def gather(slots, own, behind, panels, tiles):
    diagonals = panels.shape[0]
    any_spec = pl.BlockSpec(memory_space=pl.ANY)
    return pl.pallas_call(
        functools.partial(gather_kernel, slots),
        grid_spec=pltpu.PrefetchScalarGridSpec(
            num_scalar_prefetch=2,
            grid=(1,),
            in_specs=[any_spec, any_spec],
            out_specs=[pl.BlockSpec(memory_space=pltpu.VMEM)] * (1 + CHUNKS),
            scratch_shapes=[pltpu.SemaphoreType.DMA(((diagonals + 1) * slots,))],
        ),
        out_shape=[
            jax.ShapeDtypeStruct((diagonals, slots) + panels.shape[2:], panels.dtype),
        ] + chunk_shapes(slots, tiles),
        name="gather",
    )(own, behind, panels, tiles)


def scatter_kernel(slots, diagonal, more, behind, counts, tiles, *rest):
    returned, out, sent, sems = rest[:CHUNKS], rest[CHUNKS], rest[CHUNKS + 1:-1], rest[-1]

    def put(k):
        return pltpu.make_async_copy(
            slot_of(returned, k), out.at[behind[diagonal, k]], sems.at[k]
        )

    for k in range(slots):
        @pl.when(k < counts[1, diagonal])
        def _():
            put(k).start()
    for k in range(slots):
        @pl.when(k < counts[1, diagonal])
        def _():
            put(k).wait()
    if more:

        def take(k):
            return pltpu.make_async_copy(
                out.at[behind[diagonal + 1, k]], slot_of(sent, k), sems.at[slots + k]
            )

        for k in range(slots):
            take(k).start()
        for k in range(slots):
            take(k).wait()


def scatter(slots, diagonal, more, behind, counts, tiles, returned):
    any_spec = pl.BlockSpec(memory_space=pl.ANY)
    vmem_spec = pl.BlockSpec(memory_space=pltpu.VMEM)
    shapes = [jax.ShapeDtypeStruct(tiles.shape, tiles.dtype)]
    if more:
        shapes += chunk_shapes(slots, tiles)
    return pl.pallas_call(
        functools.partial(scatter_kernel, slots, diagonal, more),
        grid_spec=pltpu.PrefetchScalarGridSpec(
            num_scalar_prefetch=2,
            grid=(1,),
            in_specs=[any_spec] + [vmem_spec] * CHUNKS,
            out_specs=[any_spec] + [vmem_spec] * (len(shapes) - 1),
            scratch_shapes=[pltpu.SemaphoreType.DMA((2 * slots,))],
        ),
        out_shape=shapes,
        input_output_aliases={2: 0},
        name="scatter",
    )(behind, counts, tiles, *returned)


def factor_kernel(pieces_count, col_ref, *refs):
    pieces = refs[:pieces_count]
    vh_ref, vl_ref, yh_ref, yl_ref = refs[pieces_count:]
    me = col_ref[0]
    group = pieces[0].shape[1]
    band = pieces[0].shape[-1]
    depth = pieces_count * pieces[0].shape[2]
    row = lax.broadcasted_iota(jnp.int32, (depth, band), 0)
    col = lax.broadcasted_iota(jnp.int32, (depth, band), 1)
    inside = (row >= col + 1) & (row <= col + band)
    leading = row == col + 1
    r = lax.broadcasted_iota(jnp.int32, (band, band), 0)
    c = lax.broadcasted_iota(jnp.int32, (band, band), 1)
    slots = range(group)
    vs, ts, factors, inverses = [], [], [], []
    for g in slots:
        parts = [piece[0, g] for piece in pieces]
        stride = 1
        while stride < pieces_count:
            odd = (me // stride) % 2 == 1
            parts = [
                jnp.where(odd, parts[j ^ stride], parts[j]) for j in range(pieces_count)
            ]
            stride *= 2
        panel = jnp.concatenate(parts, axis=0)
        v = jnp.where(leading, 1.0, jnp.where(inside, panel, 0.0))
        vs.append(split(v))
        ts.append(split(v.T))
        vh_ref[g] = vs[g][0]
        vl_ref[g] = vs[g][1]
    for g in slots:
        gram = dot3(ts[g], vs[g])
        diagonal = jnp.sum(jnp.where(r == c, gram, 0.0), axis=0, keepdims=True)
        factors.append(gram)
        inverses.append(jnp.where(r == c, 2.0 / diagonal, 0.0))
    block = 1
    while block < band:
        coupling = (r // block != c // block) & (r // (2 * block) == c // (2 * block)) & (r < c)
        inverse_parts = [split(inverses[g]) for g in slots]
        middles = [
            split(dot3(split(jnp.where(coupling, factors[g], 0.0)), inverse_parts[g]))
            for g in slots
        ]
        inverses = [inverses[g] - dot3(inverse_parts[g], middles[g]) for g in slots]
        block *= 2
    for g in slots:
        high, low = split(dot3(split(inverses[g]), ts[g]))
        yh_ref[g] = high
        yl_ref[g] = low


def factor(slots, diagonal, col, pieces):
    count = len(pieces)
    _, _, height, band = pieces[0].shape
    depth = count * height
    group = GROUP if slots % GROUP == 0 else 1
    kind = jnp.bfloat16
    return pl.pallas_call(
        functools.partial(factor_kernel, count),
        grid_spec=pltpu.PrefetchScalarGridSpec(
            num_scalar_prefetch=1,
            grid=(slots // group,),
            in_specs=[
                pl.BlockSpec((1, group, height, band), lambda k, c: (diagonal, k, 0, 0))
            ] * count,
            out_specs=[pl.BlockSpec((group, depth, band), lambda k, c: (k, 0, 0))] * 2
            + [pl.BlockSpec((group, band, depth), lambda k, c: (k, 0, 0))] * 2,
        ),
        out_shape=[jax.ShapeDtypeStruct((slots, depth, band), kind)] * 2
        + [jax.ShapeDtypeStruct((slots, band, depth), kind)] * 2,
        name="factor",
    )(col, *pieces)


def apply_kernel(diagonal, first, own, counts, tile, below, vh, vl, yh, yl, tile_out, below_out):
    k = pl.program_id(0) + first
    band = tile.shape[1]
    upper, lower = tile[0], below[0]
    stacked = jnp.concatenate([upper, lower], axis=0)
    solved = dot3((yh[0], yl[0]), split(stacked))
    change = dot3((vh[0], vl[0]), split(solved))
    active = k < counts[0, diagonal]
    tile_out[0] = jnp.where(active, upper - change[:band], upper)
    below_out[0] = jnp.where(active, lower - change[band:], lower)


def apply(first, diagonal, own, counts, tiles, beneath, vh, vl, yh, yl):
    _, band, columns = tiles.shape
    depth = vh.shape[1]
    at_slot = lambda k, own, counts: (k, 0, 0)
    at_factor = lambda k, own, counts: (k + first, 0, 0)
    at_own = lambda k, own, counts: (own[diagonal, k + first], 0, 0)
    return pl.pallas_call(
        functools.partial(apply_kernel, diagonal, first),
        grid_spec=pltpu.PrefetchScalarGridSpec(
            num_scalar_prefetch=2,
            grid=(beneath.shape[0],),
            in_specs=[
                pl.BlockSpec((1, band, columns), at_own),
                pl.BlockSpec((1, band, columns), at_slot),
                pl.BlockSpec((1, depth, band), at_factor),
                pl.BlockSpec((1, depth, band), at_factor),
                pl.BlockSpec((1, band, depth), at_factor),
                pl.BlockSpec((1, band, depth), at_factor),
            ],
            out_specs=[
                pl.BlockSpec((1, band, columns), at_own),
                pl.BlockSpec((1, band, columns), at_slot),
            ],
        ),
        out_shape=[
            jax.ShapeDtypeStruct(tiles.shape, tiles.dtype),
            jax.ShapeDtypeStruct(beneath.shape, beneath.dtype),
        ],
        input_output_aliases={2: 0},
        name="apply",
    )(own, counts, tiles, beneath, vh, vl, yh, yl)


def lift(sent, to_above):
    beneath = []
    for chunk in sent:
        beneath.append(lax.ppermute(chunk, "row", to_above))
    return beneath


def run(slots, *args):
    return steps(slots, *args)


def steps(slots, own, behind, counts, tiles, panels):
    row_count = lax.axis_size("row")
    col_count = lax.axis_size("col")
    col = lax.axis_index("col").astype(jnp.int32)[None]
    diagonals = panels.shape[0]
    to_above = [(i, (i - 1) % row_count) for i in range(row_count)]
    to_below = [(i, (i + 1) % row_count) for i in range(row_count)]
    picked, *sent = gather(slots, own, behind, panels, tiles)
    beneath = lift(sent, to_above)
    pieces = {0: picked}
    stride = col_count // 2
    while stride >= 1:
        swap = [(i, i ^ stride) for i in range(col_count)]
        pieces.update(
            {q ^ stride: lax.ppermute(p, "col", swap) for q, p in pieces.items()}
        )
        stride //= 2
    pieces = [pieces[q] for q in range(col_count)]
    for diagonal in range(diagonals):
        factors = factor(slots, diagonal, col, pieces)
        returned = []
        for first, chunk in zip(bounds(slots), beneath):
            tiles, lower = apply(first, diagonal, own, counts, tiles, chunk, *factors)
            returned.append(lax.ppermute(lower, "row", to_below))
        more = diagonal + 1 < diagonals
        tiles, *sent = scatter(slots, diagonal, more, behind, counts, tiles, returned)
        if more:
            beneath = lift(sent, to_above)
    return tiles


def share_kernel(flags, out, held, send, recv):
    count = held.shape[0]
    me = lax.axis_index("row")
    barrier = pltpu.get_barrier_semaphore()
    mesh_id = pl.DeviceIdType.MESH
    others = [lax.rem(me + by, count) for by in range(1, count)]
    for other in others:
        pl.semaphore_signal(
            barrier, inc=1, device_id={"row": other}, device_id_type=mesh_id
        )
    pl.semaphore_wait(barrier, count - 1)
    copies = [
        pltpu.make_async_remote_copy(
            src_ref=flags,
            dst_ref=held.at[me],
            send_sem=send.at[i],
            recv_sem=recv.at[i],
            device_id={"row": other},
            device_id_type=mesh_id,
        )
        for i, other in enumerate(others)
    ]
    for copy in copies:
        copy.start()
    held[me] = flags[...]
    for copy in copies:
        copy.wait()
    out[...] = held[...]


def share(flags):
    count = lax.axis_size("row")
    diagonals, depth = flags.shape
    rows, lanes = -(-diagonals // 8) * 8, -(-depth // 128) * 128
    padded = jnp.pad(flags, ((0, rows - diagonals), (0, lanes - depth)))
    vmem_spec = pl.BlockSpec(memory_space=pltpu.VMEM)
    shape = (count, rows, lanes)
    gathered = pl.pallas_call(
        share_kernel,
        out_shape=jax.ShapeDtypeStruct(shape, flags.dtype),
        in_specs=[vmem_spec],
        out_specs=vmem_spec,
        scratch_shapes=[
            pltpu.VMEM(shape, flags.dtype),
            pltpu.SemaphoreType.DMA((count - 1,)),
            pltpu.SemaphoreType.DMA((count - 1,)),
        ],
        compiler_params=pltpu.CompilerParams(collective_id=0, has_side_effects=True),
        name="share",
    )(padded)
    return gathered[:, :diagonals, :depth]


def ordering(active):
    depth = active.shape[-1]
    here = jnp.arange(depth, dtype=jnp.int32)
    on = active.astype(jnp.int32)
    earlier = here[None, :] < here[:, None]
    before = jnp.sum(jnp.where(earlier, on[..., None, :], 0), axis=-1)
    total = jnp.sum(on, axis=-1)
    rank = jnp.where(active, before, total[..., None] + here - before)
    order = jnp.sum(
        jnp.where(rank[..., None, :] == here[:, None], here, 0), axis=-1
    ).astype(jnp.int32)
    return order, total.astype(jnp.int32)


def local(eigvec, reflectors, sweep_group):
    row_index = lax.axis_index("row")
    row_count = lax.axis_size("row")
    depth = eigvec.shape[0]
    active = share(sweep_group[:, :, 0]) >= 0
    most = jnp.max(jnp.sum(active.astype(jnp.int32), axis=-1))
    mine = lax.dynamic_index_in_dim(active, row_index, 0, keepdims=False)
    above = lax.dynamic_index_in_dim(
        active, (row_index + row_count - 1) % row_count, 0, keepdims=False
    )
    order, counts = ordering(jnp.stack([mine, above]))
    own = order[0]
    behind = jnp.where(row_index == 0, (order[1] + 1) % depth, order[1])
    sizes = [k for k in SLOT_SIZES if k < depth] + [depth]
    choice = sum((most > k).astype(jnp.int32) for k in sizes[:-1])
    branches = [functools.partial(run, k) for k in sizes]
    args = (own, behind, counts, eigvec[:, 0], reflectors[:, :, 0])
    if len(branches) == 1:
        out = branches[0](*args)
    else:
        out = lax.switch(choice, branches, *args)
    return out[:, None]


def solution(mesh):
    return jax.shard_map(
        local,
        mesh=mesh,
        in_specs=(
            P(None, "row", None, "col"),
            P(None, None, "row", "col", None),
            P(None, None, "row"),
        ),
        out_specs=P(None, "row", None, "col"),
        check_vma=False,
    )
```

profile of v0, /device:TPU:0, one launch (start us, length us, event | category | flops | bytes accessed | tf_op | source)
XLA Modules:
  0.0 221.4 jit_solution(8730782109114139389)
XLA Ops:
  0.0 4.8 %copy.125 = f32[32,1,128,256]{3,2,1,0:T(8,128)} copy(f32[32,1,128,256]{3,2,1,0:T(8,128)} %param.8) | data formatting | bytes 8388608
  4.8 0.6 pad.4.flags
  5.4 9.8 %share.1 = s32[8,8,128]{2,1,0:T(8,128)} custom-call(s32[8,128]{1,0:T(8,128)} %pad.4.flags), custom_call_target="tpu_custom_call" | custom-call | tf_op jit(solution)/shard_map/share/pallas_call | solution.py:341
  15.2 1.0 convert_reduce_fusion
  16.2 0.1 convert_reduce_fusion.1
  16.4 0.1 select_reduce_fusion.1
  16.5 0.1 subtract_select_fusion
  16.6 0.2 select_reduce_fusion
  16.7 0.7 reduce_max.9
  20.2 201.1 %conditional.1 = (f32[32,1,128,256]{3,2,1,0:T(8,128)}) conditional(s32[]{:T(128)} %clamp.3, (s32[]{:T(128)}, s32[2,2,32]{2,1,0:T(2,128)S(1)}, (), s32[2,2,32]{2,1,0:T(2,128)S(1)}, f32[32,1,128,256]{3,2,1,0:T(8,128)}, /*index=5*/f32[2,32,1,64,128]{4,3,2,1,0:T(8,128)S(1)}, s32[2,2]{1,0:T(2,128)S(1)}, ()) %tuple.64, ...), branch_computations={%region_5.6_spmd, %region_6.7_spmd, %region_7.8_spmd, %region_8.9_... | conditional | flops 835 | bytes 125830736 | solution.py:391
  20.2 0.6 slice_bitcast_fusion.1.own
  20.8 0.6 fusion.2.behind
  21.4 3.9 %gather.6 = (f32[2,12,64,128]{3,2,1,0:T(8,128)}, f32[6,128,256]{2,1,0:T(8,128)}, f32[6,128,256]{2,1,0:T(8,128)}) custom-call(s32[2,32]{1,0:T(2,128)} %slice_bitcast_fusion.1.own, s32[2,32]{1,0:T(2,128)} %fusion.2.behind, f32[2,32,64,128]{3,2,1,0:T(8,128)S(1)} %bitcast.92, f32[32,128,256]{2,1,0:T(8,128)} %bitcast.78), custom_call_target="tpu_custom_call" | custom-call | tf_op jit(solution)/shard_map/cond/branch_1_fun/gather/pallas_call | solution.py:77
  25.3 1.6 collective-permute-start.13
  26.9 0.0 collective-permute-start.12
  26.9 17.1 %collective-permute-done.13.refs_2_ = f32[2,12,64,128]{3,2,1,0:T(8,128)S(1)} collective-permute-done((f32[2,12,64,128]{3,2,1,0:T(8,128)}, f32[2,12,64,128]{3,2,1,0:T(8,128)S(1)}, u32[]{:S(2)}, u32[]{:S(2)}) %collective-permute-start.13) | collective-permute-done | bytes 786464 | tf_op jit(solution)/shard_map/cond/branch_1_fun/ppermute | solution.py:287
  44.0 0.0 collective-permute-start.14
  44.0 3.9 %collective-permute-start.11 = (f32[6,128,256]{2,1,0:T(8,128)}, f32[6,128,256]{2,1,0:T(8,128)}, u32[]{:S(2)}, u32[]{:S(2)}) collective-permute-start(f32[6,128,256]{2,1,0:T(8,128)} %get-tuple-element.293), channel_id=1, source_target_pairs={{0,28},{4,0},{8,4},{12,8},{16,12},{20,16},{24,20},{28,24},{1,29},{... | collective-permute-start | bytes 2359304 | tf_op jit(solution)/shard_map/cond/branch_1_fun/ppermute | solution.py:265
  47.9 0.5 collective-permute-start.15
  48.4 0.0 collective-permute-done.12.refs_1_
  48.4 0.0 collective-permute-done.14.refs_3_
  48.5 0.8 copy-done.9
  49.3 0.3 copy-done.10
  49.6 20.4 %factor.12 = (bf16[12,256,128]{2,1,0:T(8,128)(2,1)}, bf16[12,256,128]{2,1,0:T(8,128)(2,1)}, bf16[12,128,256]{2,1,0:T(8,128)(2,1)}, bf16[12,128,256]{2,1,0:T(8,128)(2,1)}) custom-call(s32[1]{0:T(128)} %bitcast.16.col_ref, f32[2,12,64,128]{3,2,1,0:T(8,128)} %get-tuple-element.294.refs_0_, f32[2,12,64,128]{3,2,1,0:T(8,128)} %copy-done.9, ...), custom_call_target="tpu_custom_call" | custom-call | tf_op jit(solution)/shard_map/cond/branch_1_fun/factor/pallas_call | solution.py:200
  70.0 0.0 collective-permute-done.11.below
  70.0 6.9 %apply.24 = (f32[32,128,256]{2,1,0:T(8,128)}, f32[6,128,256]{2,1,0:T(8,128)}) custom-call(s32[2,32]{1,0:T(2,128)} %slice_bitcast_fusion.1.own, s32[2,2]{1,0:T(2,128)S(1)} %get-tuple-element.289.counts, f32[32,128,256]{2,1,0:T(8,128)} %bitcast.79, f32[6,128,256]{2,1,0:T(8,128)} %collective-permute-done.11.below, ...), custom_call_target="tpu_custom_call", output_to_operand_aliasing={{0}: (2, {})} | custom-call | tf_op jit(solution)/shard_map/cond/branch_1_fun/apply/pallas_call | solution.py:235
  76.9 5.6 %collective-permute-done.15.below = f32[6,128,256]{2,1,0:T(8,128)} collective-permute-done((f32[6,128,256]{2,1,0:T(8,128)}, f32[6,128,256]{2,1,0:T(8,128)}, u32[]{:S(2)}, u32[]{:S(2)}) %collective-permute-start.15) | collective-permute-done | bytes 786464 | tf_op jit(solution)/shard_map/cond/branch_1_fun/ppermute | solution.py:265
  82.6 7.0 %apply.25 = (f32[32,128,256]{2,1,0:T(8,128)}, f32[6,128,256]{2,1,0:T(8,128)}) custom-call(s32[2,32]{1,0:T(2,128)} %slice_bitcast_fusion.1.own, s32[2,2]{1,0:T(2,128)S(1)} %get-tuple-element.289.counts, f32[32,128,256]{2,1,0:T(8,128)} %get-tuple-element.299.tile, f32[6,128,256]{2,1,0:T(8,128)} %collective-permute-done.15.below, ...), custom_call_target="tpu_custom_call", output_to_operand_aliasing={{0}: (2, {})} | custom-call | tf_op jit(solution)/shard_map/cond/branch_1_fun/apply/pallas_call | solution.py:235
  89.5 1.0 collective-permute-start.17
  90.5 0.4 collective-permute-start.16
  90.9 22.4 %collective-permute-done.17.rest_1_ = f32[6,128,256]{2,1,0:T(8,128)S(1)} collective-permute-done((f32[6,128,256]{2,1,0:T(8,128)}, f32[6,128,256]{2,1,0:T(8,128)S(1)}, u32[]{:S(2)}, u32[]{:S(2)}) %collective-permute-start.17) | collective-permute-done | bytes 786464 | tf_op jit(solution)/shard_map/cond/branch_1_fun/ppermute | solution.py:296
  113.3 15.8 %collective-permute-done.16.rest_0_ = f32[6,128,256]{2,1,0:T(8,128)S(1)} collective-permute-done((f32[6,128,256]{2,1,0:T(8,128)S(1)}, f32[6,128,256]{2,1,0:T(8,128)S(1)}, u32[]{:S(2)}, u32[]{:S(2)}) %collective-permute-start.16) | collective-permute-done | bytes 786464 | tf_op jit(solution)/shard_map/cond/branch_1_fun/ppermute | solution.py:296
  129.1 0.9 copy-done.32
  130.0 5.7 %scatter.12 = (f32[32,128,256]{2,1,0:T(8,128)}, f32[6,128,256]{2,1,0:T(8,128)}, f32[6,128,256]{2,1,0:T(8,128)}) custom-call(s32[2,32]{1,0:T(2,128)} %fusion.2.behind, s32[2,2]{1,0:T(2,128)S(1)} %get-tuple-element.289.counts, f32[32,128,256]{2,1,0:T(8,128)} %get-tuple-element.301.tiles, f32[6,128,256]{2,1,0:T(8,128)} %copy-done.32, ...), custom_call_target="tpu_custom_call", output_to_operand_aliasing={{0}: (2, {})} | custom-call | tf_op jit(solution)/shard_map/cond/branch_1_fun/scatter/pallas_call | solution.py:128
  135.7 2.0 collective-permute-start.18
  137.8 0.2 collective-permute-start.19
  138.0 20.4 %factor.13 = (bf16[12,256,128]{2,1,0:T(8,128)(2,1)}, bf16[12,256,128]{2,1,0:T(8,128)(2,1)}, bf16[12,128,256]{2,1,0:T(8,128)(2,1)}, bf16[12,128,256]{2,1,0:T(8,128)(2,1)}) custom-call(s32[1]{0:T(128)} %bitcast.16.col_ref, f32[2,12,64,128]{3,2,1,0:T(8,128)} %get-tuple-element.294.refs_0_, f32[2,12,64,128]{3,2,1,0:T(8,128)} %copy-done.9, ...), custom_call_target="tpu_custom_call" | custom-call | tf_op jit(solution)/shard_map/cond/branch_1_fun/factor/pallas_call | solution.py:200
  158.4 0.9 copy-done.30
  159.3 6.9 %apply.26 = (f32[32,128,256]{2,1,0:T(8,128)}, f32[6,128,256]{2,1,0:T(8,128)}) custom-call(s32[2,32]{1,0:T(2,128)} %slice_bitcast_fusion.1.own, s32[2,2]{1,0:T(2,128)S(1)} %get-tuple-element.289.counts, f32[32,128,256]{2,1,0:T(8,128)} %get-tuple-element.304.tile, f32[6,128,256]{2,1,0:T(8,128)} %copy-done.30, ...), custom_call_target="tpu_custom_call", output_to_operand_aliasing={{0}: (2, {})} | custom-call | tf_op jit(solution)/shard_map/cond/branch_1_fun/apply/pallas_call | solution.py:235
  166.3 5.1 %collective-permute-done.19.below = f32[6,128,256]{2,1,0:T(8,128)S(1)} collective-permute-done((f32[6,128,256]{2,1,0:T(8,128)}, f32[6,128,256]{2,1,0:T(8,128)S(1)}, u32[]{:S(2)}, u32[]{:S(2)}) %collective-permute-start.19) | collective-permute-done | bytes 786464 | tf_op jit(solution)/shard_map/cond/branch_1_fun/ppermute | solution.py:265
  171.4 0.9 copy-done.29
  172.3 7.0 %apply.27 = (f32[32,128,256]{2,1,0:T(8,128)}, f32[6,128,256]{2,1,0:T(8,128)}) custom-call(s32[2,32]{1,0:T(2,128)} %slice_bitcast_fusion.1.own, s32[2,2]{1,0:T(2,128)S(1)} %get-tuple-element.289.counts, f32[32,128,256]{2,1,0:T(8,128)} %get-tuple-element.310.tile, f32[6,128,256]{2,1,0:T(8,128)} %copy-done.29, ...), custom_call_target="tpu_custom_call", output_to_operand_aliasing={{0}: (2, {})} | custom-call | tf_op jit(solution)/shard_map/cond/branch_1_fun/apply/pallas_call | solution.py:235
  179.2 0.0 collective-permute-start.21
  179.2 0.1 collective-permute-start.20
  179.3 23.2 %collective-permute-done.21.rest_1_ = f32[6,128,256]{2,1,0:T(8,128)S(1)} collective-permute-done((f32[6,128,256]{2,1,0:T(8,128)}, f32[6,128,256]{2,1,0:T(8,128)S(1)}, u32[]{:S(2)}, u32[]{:S(2)}) %collective-permute-start.21) | collective-permute-done | bytes 786464 | tf_op jit(solution)/shard_map/cond/branch_1_fun/ppermute | solution.py:296
  202.5 14.1 %collective-permute-done.20.rest_0_ = f32[6,128,256]{2,1,0:T(8,128)S(1)} collective-permute-done((f32[6,128,256]{2,1,0:T(8,128)S(1)}, f32[6,128,256]{2,1,0:T(8,128)S(1)}, u32[]{:S(2)}, u32[]{:S(2)}) %collective-permute-start.20) | collective-permute-done | bytes 786464 | tf_op jit(solution)/shard_map/cond/branch_1_fun/ppermute | solution.py:296
  216.6 0.9 copy-done.34
  217.5 3.2 %scatter.13 = f32[32,128,256]{2,1,0:T(8,128)} custom-call(s32[2,32]{1,0:T(2,128)} %fusion.2.behind, s32[2,2]{1,0:T(2,128)S(1)} %get-tuple-element.289.counts, f32[32,128,256]{2,1,0:T(8,128)} %get-tuple-element.312.tiles, f32[6,128,256]{2,1,0:T(8,128)} %copy-done.34, f32[6,128,256]{2,1,0:T(8,128)} %copy-done.33), custom_call_target="tpu_custom_call", output_to_operand_aliasing={{}: (2, {})} | custom-call | tf_op jit(solution)/shard_map/cond/branch_1_fun/scatter/pallas_call | solution.py:128
  (24 shorter events, 0.1 us)
Async XLA Ops:
  0.0 20.2 %copy-start = (f32[2,32,1,64,128]{4,3,2,1,0:T(8,128)S(1)}, f32[2,32,1,64,128]{4,3,2,1,0:T(8,128)}, u32[]{:S(2)}) copy-start(f32[2,32,1,64,128]{4,3,2,1,0:T(8,128)} %param.9) | copy-start | bytes 6291460
  0.0 4.8 %copy-start.42 = (s32[2,32,1]{1,2,0:T(1,128)S(1)}, s32[2,32,1]{1,2,0:T(1,128)}, u32[]{:S(2)}) copy-start(s32[2,32,1]{1,2,0:T(1,128)} %param.10) | copy-start | bytes 772
  25.3 18.7 %collective-permute-start.13 = (f32[2,12,64,128]{3,2,1,0:T(8,128)}, f32[2,12,64,128]{3,2,1,0:T(8,128)S(1)}, u32[]{:S(2)}, u32[]{:S(2)}) collective-permute-start(f32[2,12,64,128]{3,2,1,0:T(8,128)} %get-tuple-element.294.refs_0_), channel_id=1, source_target_pairs={{0,2},{1,3},{2,0},{3,1},{4,6},{5,7},{6,4},{7,5},{8,10},{9,11},{10,... | collective-permute-start | bytes 2359304 | tf_op jit(solution)/shard_map/cond/branch_1_fun/ppermute | solution.py:287
  26.9 21.6 %collective-permute-start.12 = (f32[2,12,64,128]{3,2,1,0:T(8,128)}, f32[2,12,64,128]{3,2,1,0:T(8,128)S(1)}, u32[]{:S(2)}, u32[]{:S(2)}) collective-permute-start(f32[2,12,64,128]{3,2,1,0:T(8,128)} %get-tuple-element.294.refs_0_), channel_id=1, source_target_pairs={{0,1},{1,0},{2,3},{3,2},{4,5},{5,4},{6,7},{7,6},{8,9},{9,8},{10,11... | collective-permute-start | bytes 2359304 | tf_op jit(solution)/shard_map/cond/branch_1_fun/ppermute | solution.py:287
  44.0 4.5 %copy-start.8 = (f32[2,12,64,128]{3,2,1,0:T(8,128)}, f32[2,12,64,128]{3,2,1,0:T(8,128)S(1)}, u32[]{:S(2)}) copy-start(f32[2,12,64,128]{3,2,1,0:T(8,128)S(1)} %collective-permute-done.13.refs_2_) | copy-start | bytes 2359300 | tf_op jit(solution)/shard_map/cond
  44.0 4.4 %collective-permute-start.14 = (f32[2,12,64,128]{3,2,1,0:T(8,128)S(1)}, f32[2,12,64,128]{3,2,1,0:T(8,128)S(1)}, u32[]{:S(2)}, u32[]{:S(2)}) collective-permute-start(f32[2,12,64,128]{3,2,1,0:T(8,128)S(1)} %collective-permute-done.13.refs_2_), channel_id=1, source_target_pairs={{0,1},{1,0},{2,3},{3,2},{4,5},{5,4},{6,7},{7,6},{8,9},{9,8},{10,11... | collective-permute-start | bytes 2359304 | tf_op jit(solution)/shard_map/cond/branch_1_fun/ppermute | solution.py:287
  44.0 26.0 %collective-permute-start.11 = (f32[6,128,256]{2,1,0:T(8,128)}, f32[6,128,256]{2,1,0:T(8,128)}, u32[]{:S(2)}, u32[]{:S(2)}) collective-permute-start(f32[6,128,256]{2,1,0:T(8,128)} %get-tuple-element.293), channel_id=1, source_target_pairs={{0,28},{4,0},{8,4},{12,8},{16,12},{20,16},{24,20},{28,24},{1,29},{... | collective-permute-start | bytes 2359304 | tf_op jit(solution)/shard_map/cond/branch_1_fun/ppermute | solution.py:265
  47.9 34.6 %collective-permute-start.15 = (f32[6,128,256]{2,1,0:T(8,128)}, f32[6,128,256]{2,1,0:T(8,128)}, u32[]{:S(2)}, u32[]{:S(2)}) collective-permute-start(f32[6,128,256]{2,1,0:T(8,128)} %get-tuple-element.300), channel_id=1, source_target_pairs={{0,28},{4,0},{8,4},{12,8},{16,12},{20,16},{24,20},{28,24},{1,29},{... | collective-permute-start | bytes 2359304 | tf_op jit(solution)/shard_map/cond/branch_1_fun/ppermute | solution.py:265
  48.4 0.9 copy-start.9
  48.4 1.1 copy-start.10
  76.9 13.6 %copy-start.48 = (f32[6,128,256]{2,1,0:T(8,128)S(1)}, f32[6,128,256]{2,1,0:T(8,128)}, u32[]{:S(2)}) copy-start(f32[6,128,256]{2,1,0:T(8,128)} %get-tuple-element.302) | copy-start | bytes 2359300 | tf_op jit(solution)/shard_map/cond
  89.5 23.8 %collective-permute-start.17 = (f32[6,128,256]{2,1,0:T(8,128)}, f32[6,128,256]{2,1,0:T(8,128)S(1)}, u32[]{:S(2)}, u32[]{:S(2)}) collective-permute-start(f32[6,128,256]{2,1,0:T(8,128)} %get-tuple-element.303), channel_id=1, source_target_pairs={{0,4},{4,8},{8,12},{12,16},{16,20},{20,24},{24,28},{28,0},{1,5},{5... | collective-permute-start | bytes 2359304 | tf_op jit(solution)/shard_map/cond/branch_1_fun/ppermute | solution.py:296
  90.5 38.6 %collective-permute-start.16 = (f32[6,128,256]{2,1,0:T(8,128)S(1)}, f32[6,128,256]{2,1,0:T(8,128)S(1)}, u32[]{:S(2)}, u32[]{:S(2)}) collective-permute-start(f32[6,128,256]{2,1,0:T(8,128)S(1)} %copy-done.48), channel_id=1, source_target_pairs={{0,4},{4,8},{8,12},{12,16},{16,20},{20,24},{24,28},{28,0},{1,5},{5... | collective-permute-start | bytes 2359304 | tf_op jit(solution)/shard_map/cond/branch_1_fun/ppermute | solution.py:296
  113.3 15.8 %copy-start.31 = (f32[6,128,256]{2,1,0:T(8,128)}, f32[6,128,256]{2,1,0:T(8,128)S(1)}, u32[]{:S(2)}) copy-start(f32[6,128,256]{2,1,0:T(8,128)S(1)} %collective-permute-done.17.rest_1_) | copy-start | bytes 2359300 | tf_op jit(solution)/shard_map/cond
  129.1 0.9 copy-start.32
  135.7 22.7 %collective-permute-start.18 = (f32[6,128,256]{2,1,0:T(8,128)}, f32[6,128,256]{2,1,0:T(8,128)S(1)}, u32[]{:S(2)}, u32[]{:S(2)}) collective-permute-start(f32[6,128,256]{2,1,0:T(8,128)} %get-tuple-element.305), channel_id=1, source_target_pairs={{0,28},{4,0},{8,4},{12,8},{16,12},{20,16},{24,20},{28,24},{1,29},{... | collective-permute-start | bytes 2359304 | tf_op jit(solution)/shard_map/cond/branch_1_fun/ppermute | solution.py:265
  137.8 33.6 %collective-permute-start.19 = (f32[6,128,256]{2,1,0:T(8,128)}, f32[6,128,256]{2,1,0:T(8,128)S(1)}, u32[]{:S(2)}, u32[]{:S(2)}) collective-permute-start(f32[6,128,256]{2,1,0:T(8,128)} %get-tuple-element.311), channel_id=1, source_target_pairs={{0,28},{4,0},{8,4},{12,8},{16,12},{20,16},{24,20},{28,24},{1,29},{... | collective-permute-start | bytes 2359304 | tf_op jit(solution)/shard_map/cond/branch_1_fun/ppermute | solution.py:265
  158.4 0.9 copy-start.30
  166.3 13.0 %copy-start.47 = (f32[6,128,256]{2,1,0:T(8,128)S(1)}, f32[6,128,256]{2,1,0:T(8,128)}, u32[]{:S(2)}) copy-start(f32[6,128,256]{2,1,0:T(8,128)} %get-tuple-element.313) | copy-start | bytes 2359300 | tf_op jit(solution)/shard_map/cond
  171.4 0.9 copy-start.29
  179.2 23.3 %collective-permute-start.21 = (f32[6,128,256]{2,1,0:T(8,128)}, f32[6,128,256]{2,1,0:T(8,128)S(1)}, u32[]{:S(2)}, u32[]{:S(2)}) collective-permute-start(f32[6,128,256]{2,1,0:T(8,128)} %get-tuple-element.314), channel_id=1, source_target_pairs={{0,4},{4,8},{8,12},{12,16},{16,20},{20,24},{24,28},{28,0},{1,5},{5... | collective-permute-start | bytes 2359304 | tf_op jit(solution)/shard_map/cond/branch_1_fun/ppermute | solution.py:296
  179.2 37.4 %collective-permute-start.20 = (f32[6,128,256]{2,1,0:T(8,128)S(1)}, f32[6,128,256]{2,1,0:T(8,128)S(1)}, u32[]{:S(2)}, u32[]{:S(2)}) collective-permute-start(f32[6,128,256]{2,1,0:T(8,128)S(1)} %copy-done.47), channel_id=1, source_target_pairs={{0,4},{4,8},{8,12},{12,16},{16,20},{20,24},{24,28},{28,0},{1,5},{5... | collective-permute-start | bytes 2359304 | tf_op jit(solution)/shard_map/cond/branch_1_fun/ppermute | solution.py:296
  202.5 14.1 %copy-start.33 = (f32[6,128,256]{2,1,0:T(8,128)}, f32[6,128,256]{2,1,0:T(8,128)S(1)}, u32[]{:S(2)}) copy-start(f32[6,128,256]{2,1,0:T(8,128)S(1)} %collective-permute-done.21.rest_1_) | copy-start | bytes 2359300 | tf_op jit(solution)/shard_map/cond
  216.6 0.9 copy-start.34
where the time goes:
time: 222 us; the launch traced here: 221 us
  waiting for transfers between devices  103 us (46%)
  Pallas kernels  91.2 us (41%)
  local copies, waits for them, and re-layouts  10.7 us (5%)
  starting transfers between devices  9.64 us (4%)
  between operations  2.99 us (1%)
  other arithmetic  2.81 us (1%)
    ppermute x4, waiting for transfers between devices, steps(): returned.append(lax.ppermute(lower, 'row', to_below))  75.6 us
    pallas_call x2, Pallas kernels, factor(): pl.pallas_call(functools.partial(factor_kernel, count), grid_spec=pltpu.P...  40.8 us
    pallas_call x4, Pallas kernels, apply(): pl.pallas_call(functools.partial(apply_kernel, diagonal, first), grid_spe...  27.8 us
    ppermute x3, waiting for transfers between devices, steps(): lax.ppermute(p, 'col', swap)  17.1 us
    ppermute x4, waiting for transfers between devices, lift(): beneath.append(lax.ppermute(chunk, 'row', to_above))  10.7 us
    pallas_call x1, Pallas kernels, share(): pl.pallas_call(share_kernel, out_shape=jax.ShapeDtypeStruct(shape, flags....  9.77 us
    pallas_call x2, Pallas kernels, scatter(): pl.pallas_call(functools.partial(scatter_kernel, slots, diagonal, more),...  8.89 us
    ppermute x4, starting transfers between devices, lift(): beneath.append(lax.ppermute(chunk, 'row', to_above))  6.68 us
  transfers between devices with their start and end apart: 11, of which 7 were waited for; matrix products, arithmetic and copies ran while one was open for 0% of the time, Pallas kernels for 25%

commit v1 on v0

--- a/solution.py
+++ b/solution.py
@@ -8,7 +8,7 @@
 from jax.sharding import PartitionSpec as P
 
 
-SLOT_SIZES = (10, 12, 14, 16)
+SLOT_SIZES = (12, 14, 16)
 GROUP = 2
 CHUNKS = 2
 
@@ -27,7 +27,8 @@
 
 
 def bounds(slots):
-    return [slots * i // CHUNKS for i in range(CHUNKS + 1)]
+    inner = [slots * i // CHUNKS // GROUP * GROUP for i in range(CHUNKS)]
+    return inner + [slots]
 
 
 def chunk_shapes(slots, tiles):
@@ -175,27 +176,29 @@
         diagonal = jnp.sum(jnp.where(r == c, gram, 0.0), axis=0, keepdims=True)
         factors.append(gram)
         inverses.append(jnp.where(r == c, 2.0 / diagonal, 0.0))
-    block = 1
-    while block < band:
-        coupling = (r // block != c // block) & (r // (2 * block) == c // (2 * block)) & (r < c)
-        inverse_parts = [split(inverses[g]) for g in slots]
+
+    def level(n, inverses):
+        coupling = ((r >> n) != (c >> n)) & ((r >> (n + 1)) == (c >> (n + 1))) & (r < c)
+        inverse_parts = [split(inverse) for inverse in inverses]
         middles = [
             split(dot3(split(jnp.where(coupling, factors[g], 0.0)), inverse_parts[g]))
             for g in slots
         ]
-        inverses = [inverses[g] - dot3(inverse_parts[g], middles[g]) for g in slots]
-        block *= 2
+        return tuple(inverses[g] - dot3(inverse_parts[g], middles[g]) for g in slots)
+
+    inverses = lax.fori_loop(0, (band - 1).bit_length(), level, tuple(inverses))
     for g in slots:
         high, low = split(dot3(split(inverses[g]), ts[g]))
         yh_ref[g] = high
         yl_ref[g] = low
 
 
-def factor(slots, diagonal, col, pieces):
+def factor(first, slots, diagonal, col, pieces):
     count = len(pieces)
     _, _, height, band = pieces[0].shape
     depth = count * height
     group = GROUP if slots % GROUP == 0 else 1
+    start = first // group
     kind = jnp.bfloat16
     return pl.pallas_call(
         functools.partial(factor_kernel, count),
@@ -203,7 +206,7 @@
             num_scalar_prefetch=1,
             grid=(slots // group,),
             in_specs=[
-                pl.BlockSpec((1, group, height, band), lambda k, c: (diagonal, k, 0, 0))
+                pl.BlockSpec((1, group, height, band), lambda k, c: (diagonal, k + start, 0, 0))
             ] * count,
             out_specs=[pl.BlockSpec((group, depth, band), lambda k, c: (k, 0, 0))] * 2
             + [pl.BlockSpec((group, band, depth), lambda k, c: (k, 0, 0))] * 2,
@@ -230,7 +233,6 @@
     _, band, columns = tiles.shape
     depth = vh.shape[1]
     at_slot = lambda k, own, counts: (k, 0, 0)
-    at_factor = lambda k, own, counts: (k + first, 0, 0)
     at_own = lambda k, own, counts: (own[diagonal, k + first], 0, 0)
     return pl.pallas_call(
         functools.partial(apply_kernel, diagonal, first),
@@ -240,10 +242,10 @@
             in_specs=[
                 pl.BlockSpec((1, band, columns), at_own),
                 pl.BlockSpec((1, band, columns), at_slot),
-                pl.BlockSpec((1, depth, band), at_factor),
-                pl.BlockSpec((1, depth, band), at_factor),
-                pl.BlockSpec((1, band, depth), at_factor),
-                pl.BlockSpec((1, band, depth), at_factor),
+                pl.BlockSpec((1, depth, band), at_slot),
+                pl.BlockSpec((1, depth, band), at_slot),
+                pl.BlockSpec((1, band, depth), at_slot),
+                pl.BlockSpec((1, band, depth), at_slot),
             ],
             out_specs=[
                 pl.BlockSpec((1, band, columns), at_own),
@@ -289,9 +291,9 @@
         stride //= 2
     pieces = [pieces[q] for q in range(col_count)]
     for diagonal in range(diagonals):
-        factors = factor(slots, diagonal, col, pieces)
         returned = []
         for first, chunk in zip(bounds(slots), beneath):
+            factors = factor(first, chunk.shape[0], diagonal, col, pieces)
             tiles, lower = apply(first, diagonal, own, counts, tiles, chunk, *factors)
             returned.append(lax.ppermute(lower, "row", to_below))
         more = diagonal + 1 < diagonals

time: 222 us -> 222 us (level)
  waiting for transfers between devices: 103 us -> 94.5 us
  Pallas kernels: 91.2 us -> 98.9 us
    pallas_call x2 -> x4, Pallas kernels: 40.8 us -> 48.5 us  [factor(): pl.pallas_call(functools.partial(factor_kernel, count), grid_spec=pltpu.P...]
    ppermute x4, waiting for transfers between devices: 10.7 us -> 3.19 us  [lift(): beneath.append(lax.ppermute(chunk, 'row', to_above))]
  transfers between devices with their start and end apart: 11 -> 11, of which waited for: 7 -> 7; matrix products, arithmetic and copies ran while one was open for 0% -> 0% of each run, Pallas kernels for 25% -> 28%
where the time goes in v1:
time: 222 us; the launch traced here: 221 us
  Pallas kernels  98.9 us (45%)
  waiting for transfers between devices  94.5 us (43%)
  starting transfers between devices  10.9 us (5%)
  local copies, waits for them, and re-layouts  10.7 us (5%)
  other arithmetic  2.81 us (1%)
  between operations  2.32 us (1%)
    ppermute x4, waiting for transfers between devices, steps(): returned.append(lax.ppermute(lower, 'row', to_below))  74.2 us
    pallas_call x4, Pallas kernels, factor(): pl.pallas_call(functools.partial(factor_kernel, count), grid_spec=pltpu.P...  48.5 us
    pallas_call x4, Pallas kernels, apply(): pl.pallas_call(functools.partial(apply_kernel, diagonal, first), grid_spe...  27.7 us
    ppermute x3, waiting for transfers between devices, steps(): lax.ppermute(p, 'col', swap)  17.1 us
    pallas_call x1, Pallas kernels, share(): pl.pallas_call(share_kernel, out_shape=jax.ShapeDtypeStruct(shape, flags....  9.77 us
    pallas_call x2, Pallas kernels, scatter(): pl.pallas_call(functools.partial(scatter_kernel, slots, diagonal, more),...  8.89 us
    ppermute x4, starting transfers between devices, lift(): beneath.append(lax.ppermute(chunk, 'row', to_above))  6.5 us
    unnamed x5, local copies, waits for them, and re-layouts  4.82 us
  transfers between devices with their start and end apart: 11, of which 7 were waited for; matrix products, arithmetic and copies ran while one was open for 0% of the time, Pallas kernels for 28%

profile of v1, /device:TPU:0, one launch (start us, length us, event | category | flops | bytes accessed | tf_op | source)
XLA Modules:
  0.0 220.8 jit_solution(16998978978601085347)
XLA Ops:
  0.0 4.8 %copy.102 = f32[32,1,128,256]{3,2,1,0:T(8,128)} copy(f32[32,1,128,256]{3,2,1,0:T(8,128)} %param.7) | data formatting | bytes 8388608
  4.8 0.6 pad.4.flags
  5.4 9.8 %share.1 = s32[8,8,128]{2,1,0:T(8,128)} custom-call(s32[8,128]{1,0:T(8,128)} %pad.4.flags), custom_call_target="tpu_custom_call" | custom-call | tf_op jit(solution)/shard_map/share/pallas_call | solution.py:343
  15.2 1.0 convert_reduce_fusion
  16.2 0.1 convert_reduce_fusion.1
  16.3 0.1 select_reduce_fusion.1
  16.5 0.1 subtract_select_fusion
  16.6 0.2 select_reduce_fusion
  16.7 0.7 reduce_max.9
  19.5 201.0 %conditional.1 = (f32[32,1,128,256]{3,2,1,0:T(8,128)}) conditional(s32[]{:T(128)} %clamp.3, (s32[]{:T(128)}, s32[2,2,32]{2,1,0:T(2,128)S(1)}, (), s32[2,2,32]{2,1,0:T(2,128)S(1)}, f32[32,1,128,256]{3,2,1,0:T(8,128)}, /*index=5*/f32[2,32,1,64,128]{4,3,2,1,0:T(8,128)S(1)}, s32[2,2]{1,0:T(2,128)S(1)}, ()) %tuple.54, ...), branch_computations={%region_5.6_spmd, %region_6.7_spmd, %region_7.8_spmd, %region_8.9_... | conditional | flops 835 | bytes 125830736 | solution.py:393
  19.5 0.6 slice_bitcast_fusion.own
  20.1 0.6 fusion.behind
  20.7 3.9 %gather.4 = (f32[2,12,64,128]{3,2,1,0:T(8,128)}, f32[6,128,256]{2,1,0:T(8,128)}, f32[6,128,256]{2,1,0:T(8,128)}) custom-call(s32[2,32]{1,0:T(2,128)} %slice_bitcast_fusion.own, s32[2,32]{1,0:T(2,128)} %fusion.behind, f32[2,32,64,128]{3,2,1,0:T(8,128)S(1)} %bitcast.73, f32[32,128,256]{2,1,0:T(8,128)} %bitcast.61), custom_call_target="tpu_custom_call" | custom-call | tf_op jit(solution)/shard_map/cond/branch_0_fun/gather/pallas_call | solution.py:78
  24.6 1.6 collective-permute-start.2
  26.2 0.0 collective-permute-start.1
  26.2 17.1 %collective-permute-done.2.refs_2_ = f32[2,12,64,128]{3,2,1,0:T(8,128)S(1)} collective-permute-done((f32[2,12,64,128]{3,2,1,0:T(8,128)}, f32[2,12,64,128]{3,2,1,0:T(8,128)S(1)}, u32[]{:S(2)}, u32[]{:S(2)}) %collective-permute-start.2) | collective-permute-done | bytes 786464 | tf_op jit(solution)/shard_map/cond/branch_0_fun/ppermute | solution.py:289
  43.4 0.0 collective-permute-start.3
  43.4 3.9 %collective-permute-start = (f32[6,128,256]{2,1,0:T(8,128)}, f32[6,128,256]{2,1,0:T(8,128)}, u32[]{:S(2)}, u32[]{:S(2)}) collective-permute-start(f32[6,128,256]{2,1,0:T(8,128)} %get-tuple-element.214), channel_id=1, source_target_pairs={{0,28},{4,0},{8,4},{12,8},{16,12},{20,16},{24,20},{28,24},{1,29},{... | collective-permute-start | bytes 2359304 | tf_op jit(solution)/shard_map/cond/branch_0_fun/ppermute | solution.py:267
  47.3 0.5 collective-permute-start.4
  47.8 0.0 collective-permute-done.1.refs_1_
  47.8 0.9 copy-done.9
  48.7 0.3 copy-done.10
  48.9 12.1 %factor.16 = (bf16[6,256,128]{2,1,0:T(8,128)(2,1)}, bf16[6,256,128]{2,1,0:T(8,128)(2,1)}, bf16[6,128,256]{2,1,0:T(8,128)(2,1)}, bf16[6,128,256]{2,1,0:T(8,128)(2,1)}) custom-call(s32[1]{0:T(128)} %bitcast.6.col_ref, f32[2,12,64,128]{3,2,1,0:T(8,128)} %get-tuple-element.215.refs_0_, f32[2,12,64,128]{3,2,1,0:T(8,128)} %copy-done.9, ...), custom_call_target="tpu_custom_call" | custom-call | tf_op jit(solution)/shard_map/cond/branch_0_fun/factor/pallas_call | solution.py:203
  61.1 12.1 %factor.17 = (bf16[6,256,128]{2,1,0:T(8,128)(2,1)}, bf16[6,256,128]{2,1,0:T(8,128)(2,1)}, bf16[6,128,256]{2,1,0:T(8,128)(2,1)}, bf16[6,128,256]{2,1,0:T(8,128)(2,1)}) custom-call(s32[1]{0:T(128)} %bitcast.6.col_ref, f32[2,12,64,128]{3,2,1,0:T(8,128)} %get-tuple-element.215.refs_0_, f32[2,12,64,128]{3,2,1,0:T(8,128)} %copy-done.9, ...), custom_call_target="tpu_custom_call" | custom-call | tf_op jit(solution)/shard_map/cond/branch_0_fun/factor/pallas_call | solution.py:203
  73.2 6.9 %apply.16 = (f32[32,128,256]{2,1,0:T(8,128)}, f32[6,128,256]{2,1,0:T(8,128)}) custom-call(s32[2,32]{1,0:T(2,128)} %slice_bitcast_fusion.own, s32[2,2]{1,0:T(2,128)S(1)} %get-tuple-element.210.counts, f32[32,128,256]{2,1,0:T(8,128)} %bitcast.62, f32[6,128,256]{2,1,0:T(8,128)} %collective-permute-done.below, ...), custom_call_target="tpu_custom_call", output_to_operand_aliasing={{0}: (2, {})} | custom-call | tf_op jit(solution)/shard_map/cond/branch_0_fun/apply/pallas_call | solution.py:237
  80.2 1.7 collective-permute-done.4.below
  81.9 6.9 %apply.17 = (f32[32,128,256]{2,1,0:T(8,128)}, f32[6,128,256]{2,1,0:T(8,128)}) custom-call(s32[2,32]{1,0:T(2,128)} %slice_bitcast_fusion.own, s32[2,2]{1,0:T(2,128)S(1)} %get-tuple-element.210.counts, f32[32,128,256]{2,1,0:T(8,128)} %get-tuple-element.220.tile, f32[6,128,256]{2,1,0:T(8,128)} %collective-permute-done.4.below, ...), custom_call_target="tpu_custom_call", output_to_operand_aliasing={{0}: (2, {})} | custom-call | tf_op jit(solution)/shard_map/cond/branch_0_fun/apply/pallas_call | solution.py:237
  88.8 1.0 collective-permute-start.6
  89.8 0.3 collective-permute-start.5
  90.2 22.4 %collective-permute-done.6.rest_1_ = f32[6,128,256]{2,1,0:T(8,128)S(1)} collective-permute-done((f32[6,128,256]{2,1,0:T(8,128)}, f32[6,128,256]{2,1,0:T(8,128)S(1)}, u32[]{:S(2)}, u32[]{:S(2)}) %collective-permute-start.6) | collective-permute-done | bytes 786464 | tf_op jit(solution)/shard_map/cond/branch_0_fun/ppermute | solution.py:298
  112.6 15.8 %collective-permute-done.5.rest_0_ = f32[6,128,256]{2,1,0:T(8,128)S(1)} collective-permute-done((f32[6,128,256]{2,1,0:T(8,128)S(1)}, f32[6,128,256]{2,1,0:T(8,128)S(1)}, u32[]{:S(2)}, u32[]{:S(2)}) %collective-permute-start.5) | collective-permute-done | bytes 786464 | tf_op jit(solution)/shard_map/cond/branch_0_fun/ppermute | solution.py:298
  128.4 0.9 copy-done.27
  129.3 5.7 %scatter.8 = (f32[32,128,256]{2,1,0:T(8,128)}, f32[6,128,256]{2,1,0:T(8,128)}, f32[6,128,256]{2,1,0:T(8,128)}) custom-call(s32[2,32]{1,0:T(2,128)} %fusion.behind, s32[2,2]{1,0:T(2,128)S(1)} %get-tuple-element.210.counts, f32[32,128,256]{2,1,0:T(8,128)} %get-tuple-element.226.tiles, f32[6,128,256]{2,1,0:T(8,128)} %copy-done.27, ...), custom_call_target="tpu_custom_call", output_to_operand_aliasing={{0}: (2, {})} | custom-call | tf_op jit(solution)/shard_map/cond/branch_0_fun/scatter/pallas_call | solution.py:129
  135.1 2.0 collective-permute-start.7
  137.1 0.1 collective-permute-start.8
  137.1 12.1 %factor.18 = (bf16[6,256,128]{2,1,0:T(8,128)(2,1)}, bf16[6,256,128]{2,1,0:T(8,128)(2,1)}, bf16[6,128,256]{2,1,0:T(8,128)(2,1)}, bf16[6,128,256]{2,1,0:T(8,128)(2,1)}) custom-call(s32[1]{0:T(128)} %bitcast.6.col_ref, f32[2,12,64,128]{3,2,1,0:T(8,128)} %get-tuple-element.215.refs_0_, f32[2,12,64,128]{3,2,1,0:T(8,128)} %copy-done.9, ...), custom_call_target="tpu_custom_call" | custom-call | tf_op jit(solution)/shard_map/cond/branch_0_fun/factor/pallas_call | solution.py:203
  149.3 12.2 %factor.19 = (bf16[6,256,128]{2,1,0:T(8,128)(2,1)}, bf16[6,256,128]{2,1,0:T(8,128)(2,1)}, bf16[6,128,256]{2,1,0:T(8,128)(2,1)}, bf16[6,128,256]{2,1,0:T(8,128)(2,1)}) custom-call(s32[1]{0:T(128)} %bitcast.6.col_ref, f32[2,12,64,128]{3,2,1,0:T(8,128)} %get-tuple-element.215.refs_0_, f32[2,12,64,128]{3,2,1,0:T(8,128)} %copy-done.9, ...), custom_call_target="tpu_custom_call" | custom-call | tf_op jit(solution)/shard_map/cond/branch_0_fun/factor/pallas_call | solution.py:203
  161.4 0.9 copy-done.24
  162.3 6.9 %apply.18 = (f32[32,128,256]{2,1,0:T(8,128)}, f32[6,128,256]{2,1,0:T(8,128)}) custom-call(s32[2,32]{1,0:T(2,128)} %slice_bitcast_fusion.own, s32[2,2]{1,0:T(2,128)S(1)} %get-tuple-element.210.counts, f32[32,128,256]{2,1,0:T(8,128)} %get-tuple-element.229.tile, f32[6,128,256]{2,1,0:T(8,128)} %copy-done.24, ...), custom_call_target="tpu_custom_call", output_to_operand_aliasing={{0}: (2, {})} | custom-call | tf_op jit(solution)/shard_map/cond/branch_0_fun/apply/pallas_call | solution.py:237
  169.2 1.4 collective-permute-done.8.below
  170.7 0.9 copy-done.23
  171.6 6.9 %apply.19 = (f32[32,128,256]{2,1,0:T(8,128)}, f32[6,128,256]{2,1,0:T(8,128)}) custom-call(s32[2,32]{1,0:T(2,128)} %slice_bitcast_fusion.own, s32[2,2]{1,0:T(2,128)S(1)} %get-tuple-element.210.counts, f32[32,128,256]{2,1,0:T(8,128)} %get-tuple-element.235.tile, f32[6,128,256]{2,1,0:T(8,128)} %copy-done.23, ...), custom_call_target="tpu_custom_call", output_to_operand_aliasing={{0}: (2, {})} | custom-call | tf_op jit(solution)/shard_map/cond/branch_0_fun/apply/pallas_call | solution.py:237
  178.5 0.5 collective-permute-start.10
  179.1 1.0 collective-permute-start.9
  180.0 21.8 %collective-permute-done.10.rest_1_ = f32[6,128,256]{2,1,0:T(8,128)S(1)} collective-permute-done((f32[6,128,256]{2,1,0:T(8,128)}, f32[6,128,256]{2,1,0:T(8,128)S(1)}, u32[]{:S(2)}, u32[]{:S(2)}) %collective-permute-start.10) | collective-permute-done | bytes 786464 | tf_op jit(solution)/shard_map/cond/branch_0_fun/ppermute | solution.py:298
  201.8 14.1 %collective-permute-done.9.rest_0_ = f32[6,128,256]{2,1,0:T(8,128)S(1)} collective-permute-done((f32[6,128,256]{2,1,0:T(8,128)S(1)}, f32[6,128,256]{2,1,0:T(8,128)S(1)}, u32[]{:S(2)}, u32[]{:S(2)}) %collective-permute-start.9) | collective-permute-done | bytes 786464 | tf_op jit(solution)/shard_map/cond/branch_0_fun/ppermute | solution.py:298
  216.0 0.9 copy-done.30
  216.8 3.2 %scatter.9 = f32[32,128,256]{2,1,0:T(8,128)} custom-call(s32[2,32]{1,0:T(2,128)} %fusion.behind, s32[2,2]{1,0:T(2,128)S(1)} %get-tuple-element.210.counts, f32[32,128,256]{2,1,0:T(8,128)} %get-tuple-element.241.tiles, f32[6,128,256]{2,1,0:T(8,128)} %copy-done.30, f32[6,128,256]{2,1,0:T(8,128)} %copy-done.29), custom_call_target="tpu_custom_call", output_to_operand_aliasing={{}: (2, {})} | custom-call | tf_op jit(solution)/shard_map/cond/branch_0_fun/scatter/pallas_call | solution.py:129
  (26 shorter events, 0.1 us)
Async XLA Ops:
  0.0 19.5 %copy-start = (f32[2,32,1,64,128]{4,3,2,1,0:T(8,128)S(1)}, f32[2,32,1,64,128]{4,3,2,1,0:T(8,128)}, u32[]{:S(2)}) copy-start(f32[2,32,1,64,128]{4,3,2,1,0:T(8,128)} %param.8) | copy-start | bytes 6291460
  0.0 4.8 %copy-start.32 = (s32[2,32,1]{1,2,0:T(1,128)S(1)}, s32[2,32,1]{1,2,0:T(1,128)}, u32[]{:S(2)}) copy-start(s32[2,32,1]{1,2,0:T(1,128)} %param.9) | copy-start | bytes 772
  24.6 18.7 %collective-permute-start.2 = (f32[2,12,64,128]{3,2,1,0:T(8,128)}, f32[2,12,64,128]{3,2,1,0:T(8,128)S(1)}, u32[]{:S(2)}, u32[]{:S(2)}) collective-permute-start(f32[2,12,64,128]{3,2,1,0:T(8,128)} %get-tuple-element.215.refs_0_), channel_id=1, source_target_pairs={{0,2},{1,3},{2,0},{3,1},{4,6},{5,7},{6,4},{7,5},{8,10},{9,11},{10,... | collective-permute-start | bytes 2359304 | tf_op jit(solution)/shard_map/cond/branch_0_fun/ppermute | solution.py:289
  26.2 21.6 %collective-permute-start.1 = (f32[2,12,64,128]{3,2,1,0:T(8,128)}, f32[2,12,64,128]{3,2,1,0:T(8,128)S(1)}, u32[]{:S(2)}, u32[]{:S(2)}) collective-permute-start(f32[2,12,64,128]{3,2,1,0:T(8,128)} %get-tuple-element.215.refs_0_), channel_id=1, source_target_pairs={{0,1},{1,0},{2,3},{3,2},{4,5},{5,4},{6,7},{7,6},{8,9},{9,8},{10,11... | collective-permute-start | bytes 2359304 | tf_op jit(solution)/shard_map/cond/branch_0_fun/ppermute | solution.py:289
  43.4 4.5 %copy-start.8 = (f32[2,12,64,128]{3,2,1,0:T(8,128)}, f32[2,12,64,128]{3,2,1,0:T(8,128)S(1)}, u32[]{:S(2)}) copy-start(f32[2,12,64,128]{3,2,1,0:T(8,128)S(1)} %collective-permute-done.2.refs_2_) | copy-start | bytes 2359300 | tf_op jit(solution)/shard_map/cond
  43.4 4.4 %collective-permute-start.3 = (f32[2,12,64,128]{3,2,1,0:T(8,128)S(1)}, f32[2,12,64,128]{3,2,1,0:T(8,128)S(1)}, u32[]{:S(2)}, u32[]{:S(2)}) collective-permute-start(f32[2,12,64,128]{3,2,1,0:T(8,128)S(1)} %collective-permute-done.2.refs_2_), channel_id=1, source_target_pairs={{0,1},{1,0},{2,3},{3,2},{4,5},{5,4},{6,7},{7,6},{8,9},{9,8},{10,11... | collective-permute-start | bytes 2359304 | tf_op jit(solution)/shard_map/cond/branch_0_fun/ppermute | solution.py:289
  43.4 29.9 %collective-permute-start = (f32[6,128,256]{2,1,0:T(8,128)}, f32[6,128,256]{2,1,0:T(8,128)}, u32[]{:S(2)}, u32[]{:S(2)}) collective-permute-start(f32[6,128,256]{2,1,0:T(8,128)} %get-tuple-element.214), channel_id=1, source_target_pairs={{0,28},{4,0},{8,4},{12,8},{16,12},{20,16},{24,20},{28,24},{1,29},{... | collective-permute-start | bytes 2359304 | tf_op jit(solution)/shard_map/cond/branch_0_fun/ppermute | solution.py:267
  47.3 34.6 %collective-permute-start.4 = (f32[6,128,256]{2,1,0:T(8,128)}, f32[6,128,256]{2,1,0:T(8,128)}, u32[]{:S(2)}, u32[]{:S(2)}) collective-permute-start(f32[6,128,256]{2,1,0:T(8,128)} %get-tuple-element.221), channel_id=1, source_target_pairs={{0,28},{4,0},{8,4},{12,8},{16,12},{20,16},{24,20},{28,24},{1,29},{... | collective-permute-start | bytes 2359304 | tf_op jit(solution)/shard_map/cond/branch_0_fun/ppermute | solution.py:267
  47.8 0.9 copy-start.9
  47.8 1.2 copy-start.10
  80.2 9.7 %copy-start.36 = (f32[6,128,256]{2,1,0:T(8,128)S(1)}, f32[6,128,256]{2,1,0:T(8,128)}, u32[]{:S(2)}) copy-start(f32[6,128,256]{2,1,0:T(8,128)} %get-tuple-element.227) | copy-start | bytes 2359300 | tf_op jit(solution)/shard_map/cond
  88.8 23.8 %collective-permute-start.6 = (f32[6,128,256]{2,1,0:T(8,128)}, f32[6,128,256]{2,1,0:T(8,128)S(1)}, u32[]{:S(2)}, u32[]{:S(2)}) collective-permute-start(f32[6,128,256]{2,1,0:T(8,128)} %get-tuple-element.228), channel_id=1, source_target_pairs={{0,4},{4,8},{8,12},{12,16},{16,20},{20,24},{24,28},{28,0},{1,5},{5... | collective-permute-start | bytes 2359304 | tf_op jit(solution)/shard_map/cond/branch_0_fun/ppermute | solution.py:298
  89.8 38.6 %collective-permute-start.5 = (f32[6,128,256]{2,1,0:T(8,128)S(1)}, f32[6,128,256]{2,1,0:T(8,128)S(1)}, u32[]{:S(2)}, u32[]{:S(2)}) collective-permute-start(f32[6,128,256]{2,1,0:T(8,128)S(1)} %copy-done.36), channel_id=1, source_target_pairs={{0,4},{4,8},{8,12},{12,16},{16,20},{20,24},{24,28},{28,0},{1,5},{5... | collective-permute-start | bytes 2359304 | tf_op jit(solution)/shard_map/cond/branch_0_fun/ppermute | solution.py:298
  112.6 15.8 %copy-start.26 = (f32[6,128,256]{2,1,0:T(8,128)}, f32[6,128,256]{2,1,0:T(8,128)S(1)}, u32[]{:S(2)}) copy-start(f32[6,128,256]{2,1,0:T(8,128)S(1)} %collective-permute-done.6.rest_1_) | copy-start | bytes 2359300 | tf_op jit(solution)/shard_map/cond
  128.4 0.9 copy-start.27
  135.1 26.4 %collective-permute-start.7 = (f32[6,128,256]{2,1,0:T(8,128)}, f32[6,128,256]{2,1,0:T(8,128)S(1)}, u32[]{:S(2)}, u32[]{:S(2)}) collective-permute-start(f32[6,128,256]{2,1,0:T(8,128)} %get-tuple-element.230), channel_id=1, source_target_pairs={{0,28},{4,0},{8,4},{12,8},{16,12},{20,16},{24,20},{28,24},{1,29},{... | collective-permute-start | bytes 2359304 | tf_op jit(solution)/shard_map/cond/branch_0_fun/ppermute | solution.py:267
  137.1 33.6 %collective-permute-start.8 = (f32[6,128,256]{2,1,0:T(8,128)}, f32[6,128,256]{2,1,0:T(8,128)S(1)}, u32[]{:S(2)}, u32[]{:S(2)}) collective-permute-start(f32[6,128,256]{2,1,0:T(8,128)} %get-tuple-element.236), channel_id=1, source_target_pairs={{0,28},{4,0},{8,4},{12,8},{16,12},{20,16},{24,20},{28,24},{1,29},{... | collective-permute-start | bytes 2359304 | tf_op jit(solution)/shard_map/cond/branch_0_fun/ppermute | solution.py:267
  161.4 0.9 copy-start.24
  169.2 9.8 %copy-start.35 = (f32[6,128,256]{2,1,0:T(8,128)S(1)}, f32[6,128,256]{2,1,0:T(8,128)}, u32[]{:S(2)}) copy-start(f32[6,128,256]{2,1,0:T(8,128)} %get-tuple-element.242) | copy-start | bytes 2359300 | tf_op jit(solution)/shard_map/cond
  170.7 0.9 copy-start.23
  178.5 23.3 %collective-permute-start.10 = (f32[6,128,256]{2,1,0:T(8,128)}, f32[6,128,256]{2,1,0:T(8,128)S(1)}, u32[]{:S(2)}, u32[]{:S(2)}) collective-permute-start(f32[6,128,256]{2,1,0:T(8,128)} %get-tuple-element.243), channel_id=1, source_target_pairs={{0,4},{4,8},{8,12},{12,16},{16,20},{20,24},{24,28},{28,0},{1,5},{5... | collective-permute-start | bytes 2359304 | tf_op jit(solution)/shard_map/cond/branch_0_fun/ppermute | solution.py:298
  179.1 36.9 %collective-permute-start.9 = (f32[6,128,256]{2,1,0:T(8,128)S(1)}, f32[6,128,256]{2,1,0:T(8,128)S(1)}, u32[]{:S(2)}, u32[]{:S(2)}) collective-permute-start(f32[6,128,256]{2,1,0:T(8,128)S(1)} %copy-done.35), channel_id=1, source_target_pairs={{0,4},{4,8},{8,12},{12,16},{16,20},{20,24},{24,28},{28,0},{1,5},{5... | collective-permute-start | bytes 2359304 | tf_op jit(solution)/shard_map/cond/branch_0_fun/ppermute | solution.py:298
  201.8 14.1 %copy-start.29 = (f32[6,128,256]{2,1,0:T(8,128)}, f32[6,128,256]{2,1,0:T(8,128)S(1)}, u32[]{:S(2)}) copy-start(f32[6,128,256]{2,1,0:T(8,128)S(1)} %collective-permute-done.10.rest_1_) | copy-start | bytes 2359300 | tf_op jit(solution)/shard_map/cond
  215.9 0.9 copy-start.30
